TPU v7x, 128 devices: a whole 4x4x4 slice. The times are simulated.
128 devices in a mesh: dp: 16 (over y, x_lo, core), shard: 8 (over z, x_hi).
Axes of the slice: x: 4 (x_hi: 2, x_lo: 2; x = x_hi * 2 + x_lo), y: 4, z: 4, core: 2. Of those that a mesh axis runs over, the one named last changes fastest.
Arguments:
- gradients: bfloat16 [16, 88, 512, 512], P('dp', 'shard'), may hold values from -60 to 60
- owners: int32 [8, 11], P('shard'), may hold values from 0 to 15, as said below
- block_param: int32 [88], replicated, may hold values from 0 to 6, never falling along the last dimension, each value on 1 to 25 neighbouring positions
- left_stat: float32 [32, 8, 512, 512], P('dp', 'shard'), may hold values from -4 to 8, as said below
- right_stat: float32 [32, 8, 512, 512], P('dp', 'shard'), may hold values from -4 to 8, as said below
- moment: float32 [32, 8, 512, 512], P('dp', 'shard'), may hold values from 0.5 to 50
- left_root: bfloat16 [32, 8, 512, 512], P('dp', 'shard'), may hold values from -1 to 3.5, as said below
- right_root: bfloat16 [32, 8, 512, 512], P('dp', 'shard'), may hold values from -1 to 3.5, as said below
Outputs:
- new_left: float32 [32, 8, 512, 512], P('dp', 'shard')
- new_right: float32 [32, 8, 512, 512], P('dp', 'shard')
- new_moment: float32 [32, 8, 512, 512], P('dp', 'shard')
- update: bfloat16 [88, 512, 512], P('shard')
Inputs may be any that keep to these rules, and one draw needn't show every extreme that they name: `owners`: in each row, no value occurs more than 2 times, and some value occurs exactly 2 times. `left_stat`: each slot's matrix is symmetric. `right_stat`: each slot's matrix is symmetric. `left_root`: each slot's matrix is symmetric. `right_root`: each slot's matrix is symmetric.
All inputs are finite; a program needn't handle non-finite values.
Results may differ from a plain program's by a relative error of at most 0.0058.
Values may be sent and summed in bfloat16 or wider, within the bound.
A program may use at most 192 MiB of HBM per device.

v0:
```python
import jax
import jax.numpy as jnp
from jax import lax
from jax.sharding import Mesh
from jax.sharding import PartitionSpec as P

NPARAM = 7
DP = ("dp_0", "dp_1", "dp_2")
SHARD = ("shard_0", "shard_1")
DP_SHARD = ("dp_0", "dp_1", "dp_2", "shard_0", "shard_1")


decay_rate = 0.95
tiny_value = 1e-06


def by_axis(x, axes):
    for axis in axes:
        x = lax.psum(x, axis)
    return x


def on_device(gradients, owners, block_param, left_stat, right_stat, moment, left_root, right_root):
    replicas = lax.axis_size(DP)
    capacity = left_stat.shape[0]
    blocks = gradients.shape[1]
    block_width = gradients.shape[3]
    device = lax.axis_index(DP)
    column = lax.axis_index(SHARD)
    owner_row = owners[0]
    counter = jnp.arange(blocks, dtype=jnp.int32)
    same_owner = owner_row[:, None] == owner_row[None, :]
    earlier = counter[None, :] < counter[:, None]
    places = owner_row * capacity + jnp.sum(jnp.where(same_owner & earlier, 1, 0), axis=1).astype(
        jnp.int32
    )
    slot_ids = jnp.arange(replicas * capacity, dtype=jnp.int32)
    matches = places[None, :] == slot_ids[:, None]
    source = jnp.min(jnp.where(matches, counter[None, :], blocks), axis=1)
    partials = gradients[0].astype(jnp.float32)
    row_share = lax.psum_scatter(partials, DP, scatter_dimension=1, tiled=True)
    share_padded = jnp.concatenate(
        [row_share, jnp.zeros((1,) + row_share.shape[1:], jnp.float32)], axis=0
    )
    outgoing = jnp.take(share_padded, source, axis=0).reshape(
        replicas, capacity, block_width // replicas, block_width
    )
    arrived = lax.all_to_all(outgoing, DP, split_axis=0, concat_axis=2, tiled=True)
    summed = arrived[0]
    left_gram = jnp.einsum("cij,ckj->cik", summed, summed, precision=lax.Precision.HIGHEST)
    right_gram = jnp.einsum("cji,cjk->cik", summed, summed, precision=lax.Precision.HIGHEST)
    new_left = decay_rate * left_stat + (1.0 - decay_rate) * left_gram[:, None]
    new_right = decay_rate * right_stat + (1.0 - decay_rate) * right_gram[:, None]
    new_moment = decay_rate * moment + (1.0 - decay_rate) * (summed * summed)[:, None]
    adam_step = summed / (jnp.sqrt(new_moment[:, 0]) + tiny_value)
    left_half = jnp.einsum(
        "cij,cjk->cik",
        left_root[:, 0],
        summed.astype(jnp.bfloat16),
        preferred_element_type=jnp.float32,
    ).astype(jnp.bfloat16)
    direction = jnp.einsum(
        "cij,cjk->cik", left_half, right_root[:, 0], preferred_element_type=jnp.float32
    )
    my_slots = lax.dynamic_slice_in_dim(matches, device * capacity, capacity, 0)
    local_params = lax.dynamic_slice_in_dim(block_param, column * blocks, blocks, 0)
    slot_param = jnp.sum(jnp.where(my_slots, local_params[None, :], 0), axis=1)
    is_live = jnp.any(my_slots, axis=1)
    param_ids = jnp.arange(NPARAM, dtype=jnp.int32)
    member = (slot_param[:, None] == param_ids[None, :]) & is_live[:, None]
    adam_squares = jnp.sum(adam_step * adam_step, axis=(1, 2))
    direction_squares = jnp.sum(direction * direction, axis=(1, 2))
    adam_local = jnp.sum(jnp.where(member, adam_squares[:, None], 0.0), axis=0)
    direction_local = jnp.sum(jnp.where(member, direction_squares[:, None], 0.0), axis=0)
    adam_norm, direction_norm = (by_axis(adam_local, DP_SHARD), by_axis(direction_local, DP_SHARD))
    graft_ratio = jnp.sqrt((adam_norm + tiny_value) / (direction_norm + tiny_value))
    slot_ratio = jnp.sum(jnp.where(member, graft_ratio[None, :], 0.0), axis=1)
    slot_update = (slot_ratio[:, None, None] * direction).astype(jnp.bfloat16)
    returned = lax.all_to_all(slot_update, DP, split_axis=1, concat_axis=0, tiled=True)
    pieces = jnp.take(returned, places, axis=0)
    update = lax.all_gather(pieces, DP, axis=1, tiled=True)
    return (new_left, new_right, new_moment, update)


def solution(mesh):
    finer = Mesh(
        mesh.devices.reshape(4, 2, 2, 4, 2), ("dp_0", "dp_1", "dp_2", "shard_0", "shard_1")
    )
    placed = (
        P(DP, SHARD, None, None),
        P(SHARD, None),
        P(),
        P(DP, SHARD, None, None),
        P(DP, SHARD, None, None),
        P(DP, SHARD, None, None),
        P(DP, SHARD, None, None),
        P(DP, SHARD, None, None),
    )
    return jax.shard_map(
        on_device,
        mesh=finer,
        in_specs=placed,
        out_specs=(
            P(DP, SHARD, None, None),
            P(DP, SHARD, None, None),
            P(DP, SHARD, None, None),
            P(SHARD, None, None),
        ),
        check_vma=False,
    )
```

profile of v0, /device:TPU:1, one launch (start us, length us, event | category | flops | bytes accessed | tf_op | source)
XLA Modules:
  0.0 309.6 jit_solution(17516869295652060086)
XLA Ops:
  7.2 0.0 copy-start
  7.2 0.0 reduce-scatter.2.cloned.1.call-start
  7.2 8.7 %bitcast_convert_fusion = f32[11,512,512]{2,1,0:T(8,128)} fusion(bf16[1,11,512,512]{3,2,1,0:T(8,128)(2,1)} %param.8), kind=kLoop, calls=%fused_computation.2 | loop fusion | flops 2883584 | bytes 17301504 | tf_op jit(solution)/shard_map/convert_element_type | solution.py:40
  15.9 0.0 reduce-scatter.2.cloned.1.call-update
  15.9 0.6 copy-done.6
  16.6 0.2 select_reduce_fusion.1
  16.7 0.1 select_reduce_fusion
  16.9 0.1 reduce_min.14
  17.0 130.2 %reduce-scatter.2.cloned.1.call-done = f32[11,32,512]{2,1,0:T(8,128)} async-done(((f32[11,512,512]{2,1,0:T(8,128)}), f32[11,32,512]{2,1,0:T(8,128)}) %reduce-scatter.2.cloned.1.call-update) | async-done | bytes 720912 | tf_op jit(solution)/shard_map/reduce_scatter | solution.py:41
  147.2 1.2 concatenate.3
  148.4 2.0 gather_fusion
  150.4 3.1 %broadcast_select_fusion = f32[16,2,32,512]{3,2,1,0:T(8,128)} fusion(f32[16,2,32,512]{3,2,1,0:T(8,128)} %bitcast.83, pred[16,2]{1,0:T(8,128)(4,1)S(1)} %compare_and_fusion), kind=kLoop, calls=%fused_computation.23 | loop fusion | flops 524288 | bytes 4194336 | tf_op jit(solution)/shard_map/jit(_take)/select_n | solution.py:45
  153.5 5.9 %all-to-all-start = ((f32[16,2,32,512]{3,2,1,0:T(8,128)}), f32[16,2,32,512]{3,2,1,0:T(8,128)S(1)}, u32[]{:S(2)}, u32[]{:S(2)}) async-start(f32[16,2,32,512]{3,2,1,0:T(8,128)} %broadcast_select_fusion), calls=%async_computation.1 | async-start | bytes 4194304 | tf_op jit(solution)/shard_map/all_to_all | solution.py:48
  159.3 0.1 dynamic_slice.7
  159.4 0.1 fusion.15
  159.5 0.1 select_reduce_fusion.5
  159.7 26.7 %all-to-all-done = f32[16,2,32,512]{3,2,1,0:T(8,128)S(1)} async-done(((f32[16,2,32,512]{3,2,1,0:T(8,128)}), f32[16,2,32,512]{3,2,1,0:T(8,128)S(1)}, u32[]{:S(2)}, u32[]{:S(2)}) %all-to-all-start) | async-done | bytes 2097184 | tf_op jit(solution)/shard_map/all_to_all | solution.py:48
  186.4 0.3 multiply_multiply_fusion
  186.6 1.1 copy-done.2
  187.7 0.2 copy.65
  187.9 0.0 copy-start.3
  188.0 2.0 copy.61
  189.9 0.3 copy-done.3
  190.2 2.8 sqrt_add_fusion
  193.0 4.0 %multiply_reduce_fusion = (f32[2]{0:T(128)S(1)}, f32[2,512,512]{2,1,0:T(8,128)}) fusion(bf16[2,1,512,512]{3,2,1,0:T(8,128)(2,1)S(1)} %copy-done, bf16[2,1,512,512]{3,2,1,0:T(8,128)(2,1)} %param.14, f32[2,512,512]{2,1,0:T(8,128)S(1)} %bitcast.79), kind=kOutput, calls=%fused_computation.14 | convolution fusion | flops 1075838976 | bytes 6291464 | tf_op jit(solution)/shard_map/cij,cjk->cik/dot_general | solution.py:62
  197.0 2.7 fusion.3
  199.6 0.1 select_reduce_fusion.4
  199.7 7.2 %all-reduce.2 = (f32[7]{0:T(128)S(1)}, f32[7]{0:T(128)S(1)}) all-reduce(f32[7]{0:T(128)S(1)} %get-tuple-element.25, f32[7]{0:T(128)S(1)} %get-tuple-element.24), channel_id=1, replica_groups=mesh['dp_0'=4,'dp_1'=2,'dp_2'=2,'shard_0'=4,'shard_1'=2] {'dp_0'}, use_global_device_ids=true, to_apply=%region_14.15 | all-reduce | flops 14 | bytes 112 | tf_op jit(solution)/shard_map/psum | solution.py:19
  206.9 3.8 %all-reduce.5 = (f32[7]{0:T(128)S(1)}, f32[7]{0:T(128)S(1)}) all-reduce(f32[7]{0:T(128)S(1)} %get-tuple-element.28, f32[7]{0:T(128)S(1)} %get-tuple-element.29), channel_id=1, replica_groups=mesh['dp_0'=4,'dp_1'=2,'dp_2'=2,'shard_0'=4,'shard_1'=2] {'dp_1'}, use_global_device_ids=true, to_apply=%region_15.16 | all-reduce | flops 14 | bytes 112 | tf_op jit(solution)/shard_map/psum | solution.py:19
  210.7 6.2 %all-reduce.4 = (f32[7]{0:T(128)S(1)}, f32[7]{0:T(128)S(1)}) all-reduce(f32[7]{0:T(128)S(1)} %get-tuple-element.34, f32[7]{0:T(128)S(1)} %get-tuple-element.35), channel_id=1, replica_groups=mesh['dp_0'=4,'dp_1'=2,'dp_2'=2,'shard_0'=4,'shard_1'=2] {'dp_2'}, use_global_device_ids=true, to_apply=%region_16.17 | all-reduce | flops 14 | bytes 112 | tf_op jit(solution)/shard_map/psum | solution.py:19
  216.9 8.7 %all-reduce.1 = (f32[7]{0:T(128)S(1)}, f32[7]{0:T(128)S(1)}) all-reduce(f32[7]{0:T(128)S(1)} %get-tuple-element.32, f32[7]{0:T(128)S(1)} %get-tuple-element.33), channel_id=1, replica_groups=mesh['dp_0'=4,'dp_1'=2,'dp_2'=2,'shard_0'=4,'shard_1'=2] {'shard_0'}, use_global_device_ids=true, to_apply=%region_17.18 | all-reduce | flops 14 | bytes 112 | tf_op jit(solution)/shard_map/psum | solution.py:19
  225.6 5.3 %all-reduce.3 = (f32[7]{0:T(128)S(1)}, f32[7]{0:T(128)S(1)}) all-reduce(f32[7]{0:T(128)S(1)} %get-tuple-element.26, f32[7]{0:T(128)S(1)} %get-tuple-element.27), channel_id=1, replica_groups=mesh['dp_0'=4,'dp_1'=2,'dp_2'=2,'shard_0'=4,'shard_1'=2] {'shard_1'}, use_global_device_ids=true, to_apply=%region_18.19 | all-reduce | flops 14 | bytes 112 | tf_op jit(solution)/shard_map/psum | solution.py:19
  230.9 0.2 select_reduce_fusion.2
  231.1 1.9 multiply_convert_fusion
  233.0 2.0 copy.69
  235.0 7.0 %all-to-all-start.1 = ((bf16[2,512,512]{2,0,1:T(2,128)(2,1)}), bf16[2,512,512]{2,0,1:T(2,128)(2,1)S(1)}, u32[]{:S(2)}, u32[]{:S(2)}) async-start(bf16[2,512,512]{2,0,1:T(2,128)(2,1)} %copy.69), calls=%async_computation.2 | async-start | bytes 2097152 | tf_op jit(solution)/shard_map/all_to_all | solution.py:79
  242.0 0.2 all-gather.2.cloned.1.call-start
  242.2 15.5 %all-to-all-done.1 = bf16[2,512,512]{2,0,1:T(2,128)(2,1)S(1)} async-done(((bf16[2,512,512]{2,0,1:T(2,128)(2,1)}), bf16[2,512,512]{2,0,1:T(2,128)(2,1)S(1)}, u32[]{:S(2)}, u32[]{:S(2)}) %all-to-all-start.1) | async-done | bytes 1048608 | tf_op jit(solution)/shard_map/all_to_all | solution.py:79
  257.7 0.2 copy.70
  257.9 0.1 copy.71
  258.0 0.6 gather_fusion.1
  258.6 0.8 broadcast_select_fusion.1
  259.4 0.0 all-gather.2.cloned.1.call-update
  259.4 0.0 copy-start.4
  259.4 6.1 %fusion = f32[2,1,512,512]{3,2,1,0:T(8,128)} fusion(f32[2,1,512,512]{3,2,1,0:T(8,128)} %param.12, f32[2,512,512]{2,1,0:T(8,128)S(1)} %bitcast.80), kind=kOutput, calls=%fused_computation.6 | convolution fusion | flops 3222798336 | bytes 6291456 | tf_op jit(solution)/shard_map/cji,cjk->cik/dot_general | solution.py:51
  265.6 5.0 %fusion.1 = f32[2,1,512,512]{3,2,1,0:T(8,128)} fusion(f32[2,1,512,512]{3,2,1,0:T(8,128)S(1)} %copy-done.4, f32[2,512,512]{2,1,0:T(8,128)S(1)} %bitcast.81), kind=kOutput, calls=%fused_computation.9 | convolution fusion | flops 3222798336 | bytes 6291456 | tf_op jit(solution)/shard_map/cij,ckj->cik/dot_general | solution.py:50
  270.6 26.5 %all-gather.2.cloned.1.call-done = bf16[11,512,512]{2,1,0:T(8,128)(2,1)} async-done(((bf16[11,32,512]{2,1,0:T(8,128)(2,1)}), bf16[11,512,512]{2,1,0:T(8,128)(2,1)}) %all-gather.2.cloned.1.call-update) | async-done | bytes 5767184 | tf_op jit(solution)/shard_map/all_gather | solution.py:81
  297.1 5.6 %copy.85 = bf16[11,512,512]{2,1,0:T(8,128)(2,1)} copy(bf16[11,512,512]{2,1,0:T(8,128)(2,1)} %all-gather.2.cloned.1.call-done) | data formatting | bytes 11534336
  (17 shorter events, 0.1 us)
Async XLA Ops:
  7.2 185.8 %copy-start = (bf16[2,1,512,512]{3,2,1,0:T(8,128)(2,1)S(1)}, bf16[2,1,512,512]{3,2,1,0:T(8,128)(2,1)}, u32[]{:S(2)}) copy-start(bf16[2,1,512,512]{3,2,1,0:T(8,128)(2,1)} %param.15) | copy-start | bytes 3145732
  7.2 140.0 %reduce-scatter.2.cloned.1.call-start = ((), (), s32[]{:S(2)}) async-start(), calls=%async_computation.3 | async-start | bytes 12255232 | tf_op jit(solution)/shard_map/reduce_scatter | solution.py:41
  15.9 0.7 copy-start.6
  153.5 5.9 %copy-start.5 = (s32[88]{0:T(128)S(1)}, s32[88]{0:T(128)}, u32[]{:S(2)}) copy-start(s32[88]{0:T(128)} %param.10) | copy-start | bytes 1060
  153.5 32.9 %all-to-all-start = ((f32[16,2,32,512]{3,2,1,0:T(8,128)}), f32[16,2,32,512]{3,2,1,0:T(8,128)S(1)}, u32[]{:S(2)}, u32[]{:S(2)}) async-start(f32[16,2,32,512]{3,2,1,0:T(8,128)} %broadcast_select_fusion), calls=%async_computation.1 | async-start | bytes 4194304 | tf_op jit(solution)/shard_map/all_to_all | solution.py:48
  186.4 1.3 copy-start.2
  187.9 2.2 copy-start.3
  235.0 22.7 %all-to-all-start.1 = ((bf16[2,512,512]{2,0,1:T(2,128)(2,1)}), bf16[2,512,512]{2,0,1:T(2,128)(2,1)S(1)}, u32[]{:S(2)}, u32[]{:S(2)}) async-start(bf16[2,512,512]{2,0,1:T(2,128)(2,1)} %copy.69), calls=%async_computation.2 | async-start | bytes 2097152 | tf_op jit(solution)/shard_map/all_to_all | solution.py:79
  242.0 55.1 %all-gather.2.cloned.1.call-start = ((), (), s32[]{:S(2)}) async-start(), calls=%async_computation.4 | async-start | bytes 6127616 | tf_op jit(solution)/shard_map/all_gather | solution.py:81
  259.4 6.2 %copy-start.4 = (f32[2,1,512,512]{3,2,1,0:T(8,128)S(1)}, f32[2,1,512,512]{3,2,1,0:T(8,128)}, u32[]{:S(2)}) copy-start(f32[2,1,512,512]{3,2,1,0:T(8,128)} %param.11) | copy-start | bytes 6291460
  297.1 5.6 %copy-start.1 = (bf16[2,1,512,512]{3,2,1,0:T(8,128)(2,1)S(1)}, bf16[2,1,512,512]{3,2,1,0:T(8,128)(2,1)}, u32[]{:S(2)}) copy-start(bf16[2,1,512,512]{3,2,1,0:T(8,128)(2,1)} %param.15) | copy-start | bytes 3145732
Sparse Core Ops, SparseCore 0:
  16.0 131.0 reduce-scatter.1
  259.6 37.5 all-gather.1
where the time goes:
time: 310 us
  waiting for transfers between devices  199 us (64%)
  blocking collectives  31.1 us (10%)
  other arithmetic  21.1 us (7%)
  local copies, waits for them, and re-layouts  16 us (5%)
  matrix products  15.1 us (5%)
  between operations  14.2 us (5%)
  starting transfers between devices  13.1 us (4%)
    reduce_scatter x1, waiting for transfers between devices, on_device(): row_share = lax.psum_scatter(partials, DP, scatter_dimension=1, tiled=True)  130 us
    psum x5, blocking collectives, by_axis(): x = lax.psum(x, axis)  31.1 us
    all_to_all x1, waiting for transfers between devices, on_device(): lax.all_to_all(outgoing, DP, split_axis=0, concat_axis=2, tiled=True)  26.7 us
    all_gather x1, waiting for transfers between devices, on_device(): update = lax.all_gather(pieces, DP, axis=1, tiled=True)  26.5 us
    all_to_all x1, waiting for transfers between devices, on_device(): lax.all_to_all(slot_update, DP, split_axis=1, concat_axis=0, tiled=True)  15.5 us
    convert_element_type x1, other arithmetic, on_device(): partials = gradients[0].astype(jnp.float32)  8.67 us
    unnamed x15, local copies, waits for them, and re-layouts  7.59 us
    all_to_all x1, starting transfers between devices, on_device(): lax.all_to_all(slot_update, DP, split_axis=1, concat_axis=0, tiled=True)  6.96 us
  transfers between devices with their start and end apart: 4, of which 4 were waited for; matrix products, arithmetic and copies ran while one was open for 4% of the time, Pallas kernels for 0%

commit v1 on v0

v1 whole, which is shorter than its diff:
```python
import functools

import jax
import jax.numpy as jnp
from jax import lax
from jax.experimental import pallas as pl
from jax.experimental.pallas import tpu as pltpu
from jax.sharding import PartitionSpec as P

NPARAM = 7
DECAY = 0.95
TINY = 1e-06
NY, NX, NC = 4, 2, 2
BF = jnp.bfloat16
F32 = jnp.float32


def position():
    d = lax.axis_index("dp")
    return d // 4, (d // 2) % 2, d % 2


def flat(y, x, c):
    return (y % NY) * 4 + (x % NX) * 2 + c % NC


OFFSETS = [
    (dy, dx, dc)
    for dy in (2, 1, 3, 0)
    for dx in (1, 0)
    for dc in (0, 1)
    if (dy, dx, dc) != (0, 0, 0)
]


class Copies:
    def __init__(self, send, recv):
        self.send, self.recv, self.count, self.all = send, recv, 0, []

    def start(self, src, dst, where):
        i = self.count
        self.count += 1
        copy = pltpu.make_async_remote_copy(
            src_ref=src,
            dst_ref=dst,
            send_sem=self.send.at[i],
            recv_sem=self.recv.at[i],
            device_id=where,
            device_id_type=pl.DeviceIdType.MESH,
        )
        copy.start()
        self.all.append(copy)
        return copy

    def finish(self):
        for copy in self.all:
            copy.wait_send()


def add_blocks(count, out, first, second):
    def body(b, carry):
        out[b] = first[b] + second[b]
        return carry

    lax.fori_loop(0, count, body, 0)


def add_many(count, out, *terms):
    def body(b, carry):
        total = terms[0][b].astype(F32)
        for term in terms[1:]:
            total = total + term[b].astype(F32)
        out[b] = total.astype(BF)
        return carry

    lax.fori_loop(0, count, body, 0)


def reduce_kernel(
    nblk, na_blk, source_ref, grad_ref, held_ref, loc, rem, far_a, mid_b, near_a, mid_a,
    far_b, near_b, share, stage, local_sem, send_sem, recv_sem,
):
    y, x, c = position()
    nb_blk = nblk - na_blk
    rows = share.shape[1]
    half = rows // 2
    ox, oc = 1 - x, 1 - c
    up, down, across = (y + 1) % NY, (y + 3) % NY, (y + 2) % NY
    A = pl.ds(0, na_blk)
    B = pl.ds(na_blk, nb_blk)
    H = (pl.ds(0, half), pl.ds(half, half))

    def gpart(which, core):
        return [
            grad_ref.at[A, core, across],
            grad_ref.at[B, core, :, ox],
            grad_ref.at[A, core, up],
            grad_ref.at[A, core, down],
            grad_ref.at[B, core, :, x],
            grad_ref.at[A, core, y],
        ][which]

    def vpart(buf, which):
        return [
            buf.at[A, across],
            buf.at[B, :, ox],
            buf.at[A, up],
            buf.at[A, down],
            buf.at[B, :, x],
            buf.at[A, y],
        ][which]

    loads = []
    for i in range(6):
        load = pltpu.make_async_copy(gpart(i, c), vpart(loc, i), local_sem.at[i])
        load.start()
        loads.append(load)

    barrier = pltpu.get_barrier_semaphore()
    for dy, dx, dc in OFFSETS:
        pl.semaphore_signal(
            barrier, inc=1, device_id={"dp": flat(y + dy, x + dx, c + dc)},
            device_id_type=pl.DeviceIdType.MESH,
        )
    pl.semaphore_wait(barrier, len(OFFSETS))

    to_core = {"dp": flat(y, x, oc)}
    to_x = {"dp": flat(y, ox, c)}
    to_up = {"dp": flat(up, x, c)}
    to_down = {"dp": flat(down, x, c)}
    copies = Copies(send_sem, recv_sem)
    pair = [copies.start(gpart(i, oc), vpart(rem, i), to_core) for i in range(6)]

    def pair_sum(i):
        loads[i].wait()
        pair[i].wait_recv()
        mine, other = vpart(loc, i), vpart(rem, i)
        inner = mine.shape[1]
        for j in range(inner):
            add_blocks(
                mine.shape[0], mine.at[:, j], mine.at[:, j], other.at[:, j]
            )

    pair_sum(0)
    fa = [
        copies.start(loc.at[A, across, 0], far_a.at[0], to_up),
        copies.start(loc.at[A, across, 1], far_a.at[1], to_down),
    ]
    pair_sum(1)
    mb = [
        copies.start(loc.at[B, chunk, ox], mid_b.at[:, chunk], to_x)
        for chunk in (across, up, down, y)
    ]
    pair_sum(2)
    n_a = {(0, 1): copies.start(loc.at[A, up, 1], near_a.at[0, 1], to_up)}
    pair_sum(3)
    n_a[1, 0] = copies.start(loc.at[A, down, 0], near_a.at[1, 0], to_down)
    pair_sum(4)
    pair_sum(5)

    fa[0].wait_recv()
    add_blocks(na_blk, loc.at[A, up, 0], loc.at[A, up, 0], far_a.at[0])
    n_a[0, 0] = copies.start(loc.at[A, up, 0], near_a.at[0, 0], to_up)
    fa[1].wait_recv()
    add_blocks(na_blk, loc.at[A, down, 1], loc.at[A, down, 1], far_a.at[1])
    n_a[1, 1] = copies.start(loc.at[A, down, 1], near_a.at[1, 1], to_down)

    def middle(i, chunk):
        mb[i].wait_recv()
        add_blocks(nb_blk, loc.at[B, chunk, x], loc.at[B, chunk, x], mid_b.at[:, chunk])

    middle(0, across)
    fb = [
        copies.start(loc.at[B, across, x, H[0]], far_b.at[0], to_up),
        copies.start(loc.at[B, across, x, H[1]], far_b.at[1], to_down),
    ]
    middle(1, up)
    n_b = {(0, 1): copies.start(loc.at[B, up, x, H[1]], near_b.at[0, 1], to_up)}
    middle(2, down)
    n_b[1, 0] = copies.start(loc.at[B, down, x, H[0]], near_b.at[1, 0], to_down)

    for key in ((0, 1), (1, 0), (0, 0), (1, 1)):
        n_a[key].wait_recv()
    add_many(na_blk, loc.at[A, y, ox], loc.at[A, y, ox], near_a.at[0, ox], near_a.at[1, ox])
    ma = copies.start(loc.at[A, y, ox], mid_a, to_x)

    fb[0].wait_recv()
    add_blocks(nb_blk, loc.at[B, up, x, H[0]], loc.at[B, up, x, H[0]], far_b.at[0])
    n_b[0, 0] = copies.start(loc.at[B, up, x, H[0]], near_b.at[0, 0], to_up)
    fb[1].wait_recv()
    add_blocks(nb_blk, loc.at[B, down, x, H[1]], loc.at[B, down, x, H[1]], far_b.at[1])
    n_b[1, 1] = copies.start(loc.at[B, down, x, H[1]], near_b.at[1, 1], to_down)

    share[nblk] = jnp.zeros(share.shape[1:], BF)
    ma.wait_recv()
    add_many(
        na_blk, share.at[A], loc.at[A, y, x], near_a.at[0, x], near_a.at[1, x], mid_a
    )
    mb[3].wait_recv()
    for key in ((0, 1), (1, 0), (0, 0), (1, 1)):
        n_b[key].wait_recv()
    for h in range(2):
        add_many(
            nb_blk, share.at[B, H[h]], loc.at[B, y, x, H[h]], mid_b.at[:, y, H[h]],
            near_b.at[0, h], near_b.at[1, h],
        )

    sent = []
    for k, (dy, dx, dc) in enumerate(OFFSETS):
        q = flat(y + dy, x + dx, c + dc)
        for j in range(2):
            stage[k, j] = share[source_ref[q * 2 + j]]
        sent.append(copies.start(stage.at[k], held_ref.at[:, c, y, x], {"dp": q}))
    mine = flat(y, x, c)
    for j in range(2):
        held_ref[j, c, y, x] = share[source_ref[mine * 2 + j]]
    for copy in sent:
        copy.wait_recv()
    copies.finish()


def reduce_to_owners(gradients, source):
    nblk, block, width = gradients.shape
    rows = block // (NY * NX * NC)
    na_blk = (nblk + 1) // 2
    nb_blk = nblk - na_blk
    n_copies = 6 + 2 + 4 + 4 + 2 + 4 + 1 + len(OFFSETS)
    held = pl.pallas_call(
        functools.partial(reduce_kernel, nblk, na_blk),
        out_shape=jax.ShapeDtypeStruct((2, NC, NY, NX, rows, width), BF),
        in_specs=[
            pl.BlockSpec(memory_space=pltpu.SMEM),
            pl.BlockSpec(memory_space=pl.ANY),
        ],
        out_specs=pl.BlockSpec(memory_space=pltpu.VMEM),
        scratch_shapes=[
            pltpu.VMEM((nblk, NY, NX, rows, width), BF),
            pltpu.VMEM((nblk, NY, NX, rows, width), BF),
            pltpu.VMEM((2, na_blk, rows, width), BF),
            pltpu.VMEM((nb_blk, NY, rows, width), BF),
            pltpu.VMEM((2, 2, na_blk, rows, width), BF),
            pltpu.VMEM((na_blk, rows, width), BF),
            pltpu.VMEM((2, nb_blk, rows // 2, width), BF),
            pltpu.VMEM((2, 2, nb_blk, rows // 2, width), BF),
            pltpu.VMEM((nblk + 1, rows, width), BF),
            pltpu.VMEM((len(OFFSETS), 2, rows, width), BF),
            pltpu.SemaphoreType.DMA((6,)),
            pltpu.SemaphoreType.DMA((n_copies,)),
            pltpu.SemaphoreType.DMA((n_copies,)),
        ],
        compiler_params=pltpu.CompilerParams(collective_id=0, has_side_effects=True),
        name="reduce_to_owners",
    )(source, gradients.reshape(nblk, NC, NY, NX, rows, width))
    return held.reshape(2, block, width)


def slot_kernel(
    param_ref, held_ref, lroot_ref, rroot_ref, lstat_ref, rstat_ref, moment_ref,
    nl_ref, nr_ref, nm_ref, dir_ref, norm_ref, acc,
):
    s, r = pl.program_id(0), pl.program_id(1)
    step = lstat_ref.shape[1]
    at = pl.multiple_of(r * step, step)
    held = held_ref[0]
    part = held_ref[0, pl.ds(at, step), :]
    columns = held_ref[0, :, pl.ds(at, step)]
    left = lax.dot_general(part, held, (((1,), (1,)), ((), ())), preferred_element_type=F32)
    nl_ref[0] = DECAY * lstat_ref[0] + (1.0 - DECAY) * left
    right = lax.dot_general(columns, held, (((0,), (0,)), ((), ())), preferred_element_type=F32)
    nr_ref[0] = DECAY * rstat_ref[0] + (1.0 - DECAY) * right
    wide = part.astype(F32)
    moment = DECAY * moment_ref[0] + (1.0 - DECAY) * (wide * wide)
    nm_ref[0] = moment
    adam = wide / (jnp.sqrt(moment) + TINY)
    first = jnp.dot(lroot_ref[0], held, preferred_element_type=F32)
    high = first.astype(BF)
    low = (first - high.astype(F32)).astype(BF)
    direction = jnp.dot(high, rroot_ref[0], preferred_element_type=F32)
    direction += jnp.dot(low, rroot_ref[0], preferred_element_type=F32)
    dir_ref[0] = direction.astype(BF)
    width = wide.shape[1]

    @pl.when(r == 0)
    def _():
        acc[...] = jnp.zeros_like(acc)

    acc[0] += jnp.sum((adam * adam).reshape(step // 8, 8, width), axis=0)
    acc[1] += jnp.sum((direction * direction).reshape(step // 8, 8, width), axis=0)

    @pl.when((s == 0) & (r == 0))
    def _():
        norm_ref[...] = jnp.zeros_like(norm_ref)

    @pl.when(r == pl.num_programs(1) - 1)
    def _():
        row = lax.broadcasted_iota(jnp.int32, norm_ref.shape, 0)
        lane = lax.broadcasted_iota(jnp.int32, norm_ref.shape, 1)
        here = lane == param_ref[s]
        total = jnp.where(row == 0, jnp.sum(acc[0]), jnp.sum(acc[1]))
        norm_ref[...] += jnp.where(here & (row < 2), total, 0.0)


def slot_step(slot_param, held, lroot, rroot, lstat, rstat, moment):
    slots, block, width = held.shape
    step = min(128, block)
    whole = pl.BlockSpec((1, block, width), lambda s, r: (s, 0, 0))
    strip = pl.BlockSpec((1, step, width), lambda s, r: (s, r, 0))
    big = jax.ShapeDtypeStruct((slots, block, width), F32)
    return pl.pallas_call(
        slot_kernel,
        grid=(slots, block // step),
        out_shape=(
            big, big, big,
            jax.ShapeDtypeStruct((slots, block, width), BF),
            jax.ShapeDtypeStruct((8, 128), F32),
        ),
        in_specs=[
            pl.BlockSpec(memory_space=pltpu.SMEM), whole, strip, whole, strip, strip, strip,
        ],
        out_specs=(strip, strip, strip, strip, pl.BlockSpec((8, 128), lambda s, r: (0, 0))),
        scratch_shapes=[pltpu.VMEM((2, 8, width), F32)],
        compiler_params=pltpu.CompilerParams(dimension_semantics=("arbitrary", "arbitrary")),
        name="slot_step",
    )(slot_param, held, lroot, rroot, lstat, rstat, moment)


def gather_kernel(
    nblk, na_blk, n_shard, place_ref, norm_ref, dir_ref, out_ref, total_ref,
    slots, norms, group, columns, send_sem, recv_sem,
):
    y, x, c = position()
    mine = flat(y, x, c)
    shard = lax.axis_index("shard")
    nb_blk = nblk - na_blk
    rows = slots.shape[2]
    half = rows // 2
    ox, oc = 1 - x, 1 - c
    up, down, across = (y + 1) % NY, (y + 3) % NY, (y + 2) % NY
    A = pl.ds(0, na_blk)
    B = pl.ds(na_blk, nb_blk)
    ALL = pl.ds(0, nblk)
    H = (pl.ds(0, half), pl.ds(half, half))

    barrier = pltpu.get_barrier_semaphore()
    for dy, dx, dc in OFFSETS:
        pl.semaphore_signal(
            barrier, inc=1, device_id={"dp": flat(y + dy, x + dx, c + dc)},
            device_id_type=pl.DeviceIdType.MESH,
        )
    for k in range(1, n_shard):
        pl.semaphore_signal(
            barrier, inc=1, device_id={"shard": (shard + k) % n_shard},
            device_id_type=pl.DeviceIdType.MESH,
        )
    pl.semaphore_wait(barrier, len(OFFSETS) + n_shard - 1)

    copies = Copies(send_sem, recv_sem)
    first, second = [], []
    for dy, dx, dc in OFFSETS:
        q = flat(y + dy, x + dx, c + dc)
        first.append(copies.start(norm_ref, norms.at[mine], {"dp": q}))
    for dy, dx, dc in OFFSETS:
        qy, qx, qc = (y + dy) % NY, (x + dx) % NX, (c + dc) % NC
        second.append(
            copies.start(dir_ref.at[:, qc, qy, qx], slots.at[mine], {"dp": flat(qy, qx, qc)})
        )
    norms[mine] = norm_ref[...]
    slots[mine] = dir_ref[:, c, y, x]
    for copy in first:
        copy.wait_recv()
    total = norms[0]
    for i in range(1, norms.shape[0]):
        total = total + norms[i]
    group[...] = total
    third = [
        copies.start(group, columns.at[shard], {"shard": (shard + k) % n_shard})
        for k in range(1, n_shard)
    ]
    columns[shard] = total

    for copy in second:
        copy.wait_recv()
    for b in range(nblk):
        place = place_ref[b]
        out_ref[b, c, y, x] = slots[place // 2, place % 2]

    to_core = {"dp": flat(y, x, oc)}
    to_x = {"dp": flat(y, ox, c)}
    to_up = {"dp": flat(up, x, c)}
    to_down = {"dp": flat(down, x, c)}
    arrivals = []

    def pass_on(where, *index):
        part = out_ref.at[index]
        return copies.start(part, part, where)

    def across_cores(*index):
        arrivals.append(pass_on(to_core, *index))

    xa = pass_on(to_x, A, c, y, x)
    b_near = [pass_on(to_up, B, c, y, x), pass_on(to_down, B, c, y, x)]
    xb = [pass_on(to_x, B, c, y, x)]
    a_near = [pass_on(to_up, A, c, y, x), pass_on(to_down, A, c, y, x)]
    across_cores(ALL, c, y, x)

    b_near[0].wait_recv()
    b_far = [pass_on(to_up, B, c, down, x, H[0])]
    xb.append(pass_on(to_x, B, c, down, x))
    b_near[1].wait_recv()
    b_far.append(pass_on(to_down, B, c, up, x, H[1]))
    xb.append(pass_on(to_x, B, c, up, x))
    across_cores(B, c, down, x)
    across_cores(B, c, up, x)

    xa.wait_recv()
    a_next = [pass_on(to_up, A, c, y, ox), pass_on(to_down, A, c, y, ox)]
    across_cores(A, c, y, ox)

    a_near[0].wait_recv()
    a_far = [pass_on(to_up, A, c, down, x)]
    across_cores(A, c, down, x)
    a_near[1].wait_recv()
    across_cores(A, c, up, x)

    b_far[0].wait_recv()
    b_far[1].wait_recv()
    xb.append(pass_on(to_x, B, c, across, x))
    across_cores(B, c, across, x)

    a_next[1].wait_recv()
    a_far.append(pass_on(to_down, A, c, up, ox))
    across_cores(A, c, up, ox)
    a_next[0].wait_recv()
    across_cores(A, c, down, ox)

    for copy in third:
        copy.wait_recv()
    total = columns[0]
    for i in range(1, n_shard):
        total = total + columns[i]
    total_ref[...] = total

    for i, chunk in enumerate((y, down, up)):
        xb[i].wait_recv()
        across_cores(B, c, chunk, ox)
    a_far[0].wait_recv()
    across_cores(A, c, across, x)
    a_far[1].wait_recv()
    across_cores(A, c, across, ox)
    xb[3].wait_recv()
    across_cores(B, c, across, ox)
    for copy in arrivals:
        copy.wait_recv()
    copies.finish()


def gather_blocks(direction, places, norm, n_shard):
    slots, block, width = direction.shape
    nblk = places.shape[0]
    rows = block // (NY * NX * NC)
    na_blk = (nblk + 1) // 2
    n_dev = NY * NX * NC
    n_copies = 2 * len(OFFSETS) + n_shard - 1 + 1 + 2 + 4 + 2 + 2 + 2 + 2 + 15
    out, total = pl.pallas_call(
        functools.partial(gather_kernel, nblk, na_blk, n_shard),
        out_shape=(
            jax.ShapeDtypeStruct((nblk, NC, NY, NX, rows, width), BF),
            jax.ShapeDtypeStruct(norm.shape, F32),
        ),
        in_specs=[
            pl.BlockSpec(memory_space=pltpu.SMEM),
            pl.BlockSpec(memory_space=pltpu.VMEM),
            pl.BlockSpec(memory_space=pltpu.VMEM),
        ],
        out_specs=(
            pl.BlockSpec(memory_space=pltpu.VMEM),
            pl.BlockSpec(memory_space=pltpu.VMEM),
        ),
        scratch_shapes=[
            pltpu.VMEM((n_dev, slots, rows, width), BF),
            pltpu.VMEM((n_dev,) + norm.shape, F32),
            pltpu.VMEM(norm.shape, F32),
            pltpu.VMEM((n_shard,) + norm.shape, F32),
            pltpu.SemaphoreType.DMA((n_copies,)),
            pltpu.SemaphoreType.DMA((n_copies,)),
        ],
        compiler_params=pltpu.CompilerParams(collective_id=1, has_side_effects=True),
        name="gather_blocks",
    )(places, norm, direction.reshape(slots, NC, NY, NX, rows, width))
    return out.reshape(nblk, block, width), total


def on_device(gradients, owners, block_param, left_stat, right_stat, moment, left_root, right_root):
    replicas = lax.axis_size("dp")
    n_shard = lax.axis_size("shard")
    capacity = left_stat.shape[0]
    blocks = gradients.shape[1]
    device = lax.axis_index("dp")
    column = lax.axis_index("shard")
    owner_row = owners[0]
    counter = jnp.arange(blocks, dtype=jnp.int32)
    same_owner = owner_row[:, None] == owner_row[None, :]
    earlier = counter[None, :] < counter[:, None]
    places = owner_row * capacity + jnp.sum(
        jnp.where(same_owner & earlier, 1, 0), axis=1
    ).astype(jnp.int32)
    slot_ids = jnp.arange(replicas * capacity, dtype=jnp.int32)
    matches = places[None, :] == slot_ids[:, None]
    source = jnp.min(jnp.where(matches, counter[None, :], blocks), axis=1)
    local_params = lax.dynamic_slice_in_dim(block_param, column * blocks, blocks, 0)
    my_ids = device * capacity + jnp.arange(capacity, dtype=jnp.int32)
    mine = places[None, :] == my_ids[:, None]
    slot_param = jnp.max(jnp.where(mine, local_params[None, :], -1), axis=1)

    held = reduce_to_owners(gradients[0], source)
    new_left, new_right, new_moment, direction, norm = slot_step(
        slot_param, held, left_root[:, 0], right_root[:, 0],
        left_stat[:, 0], right_stat[:, 0], moment[:, 0],
    )
    gathered, total = gather_blocks(direction, places, norm, n_shard)
    graft_ratio = jnp.sqrt((total[0, :NPARAM] + TINY) / (total[1, :NPARAM] + TINY))
    param_ids = jnp.arange(NPARAM, dtype=jnp.int32)
    member = local_params[:, None] == param_ids[None, :]
    block_ratio = jnp.sum(jnp.where(member, graft_ratio[None, :], 0.0), axis=1)
    update = (block_ratio[:, None, None] * gathered.astype(F32)).astype(BF)
    return (new_left[:, None], new_right[:, None], new_moment[:, None], update)


def solution(mesh):
    state = P("dp", "shard", None, None)
    return jax.shard_map(
        on_device,
        mesh=mesh,
        in_specs=(state, P("shard", None), P(), state, state, state, state, state),
        out_specs=(state, state, state, P("shard", None, None)),
        check_vma=False,
    )
```

time: 310 us -> 118 us (0.38)
  waiting for transfers between devices: 199 us -> 0 us
  Pallas kernels: 0 us -> 104 us
  blocking collectives: 31.1 us -> 0 us
  local copies, waits for them, and re-layouts: 16 us -> 0.74 us
  matrix products: 15.1 us -> 0 us
  between operations: 14.2 us -> 0.66 us
  starting transfers between devices: 13.1 us -> 0 us
  other arithmetic: 21.1 us -> 11.9 us
    reduce_scatter x1 -> x0, waiting for transfers between devices: 130 us -> none  [on_device(): row_share = lax.psum_scatter(partials, DP, scatter_dimension=1, tiled=True)]
    pallas_call x0 -> x3, Pallas kernels: none -> 104 us  [the longest x1 48.6 us: gather_blocks(): pl.pallas_call(functools.partial(gather_kernel, nblk, na_blk, n_shard), o...]
    all_to_all x2 -> x0, waiting for transfers between devices: 42.2 us -> none  [the longest x1 26.7 us: on_device(): lax.all_to_all(outgoing, DP, split_axis=0, concat_axis=2, tiled=True)]
    psum x5 -> x0, blocking collectives: 31.1 us -> none  [by_axis(): x = lax.psum(x, axis)]
    all_gather x1 -> x0, waiting for transfers between devices: 26.5 us -> none  [on_device(): update = lax.all_gather(pieces, DP, axis=1, tiled=True)]
    dot_general x3 -> x0, matrix products: 15.1 us -> none  [the longest x1 6.14 us: on_device(): jnp.einsum('cji,cjk->cik', summed, summed, precision=lax.Precision.HIGHEST)]
    all_to_all x2 -> x0, starting transfers between devices: 12.8 us -> none  [the longest x1 6.96 us: on_device(): lax.all_to_all(slot_update, DP, split_axis=1, concat_axis=0, tiled=True)]
    unnamed x15 -> x0, local copies, waits for them, and re-layouts: 7.59 us -> none
  transfers between devices with their start and end apart: 4 -> 0, of which waited for: 4 -> 0; matrix products, arithmetic and copies ran while one was open for 4% -> 0% of each run, Pallas kernels for 0% -> 0%
where the time goes in v1:
time: 118 us; the launch traced here: 117 us
  Pallas kernels  104 us (88%)
  other arithmetic  11.9 us (10%)
    pallas_call x1, Pallas kernels, gather_blocks(): pl.pallas_call(functools.partial(gather_kernel, nblk, na_blk, n_shard), o...  48.6 us
    pallas_call x1, Pallas kernels, reduce_to_owners(): pl.pallas_call(functools.partial(reduce_kernel, nblk, na_blk), out_shape=...  43.8 us
    pallas_call x1, Pallas kernels, slot_step(): pl.pallas_call(slot_kernel, grid=(slots, block // step), out_shape=(big,...  11.5 us
    convert_element_type x1, other arithmetic, on_device(): update = (block_ratio[:, None, None] * gathered.astype(F32)).astype(BF)  6.93 us

profile of v1, /device:TPU:1, one launch (start us, length us, event | category | flops | bytes accessed | tf_op | source)
XLA Modules:
  0.0 117.2 jit_solution(10064632302229630015)
XLA Ops:
  0.6 0.7 dynamic_slice.3
  1.4 0.9 select_reduce_fusion.1
  2.3 0.7 fusion.3
  3.0 1.2 %multiply_add_fusion.place_ref = s32[11]{0:T(128)} fusion(s32[11]{0:T(128)S(1)} %select_reduce_fusion.1, s32[1,11]{1,0:T(1,128)} %param.9), kind=kLoop, calls=%fused_computation.15 | loop fusion | flops 22 | bytes 132 | tf_op jit(solution)/shard_map/add | solution.py:504
  4.2 0.7 fusion.2.param_ref
  4.9 0.6 select_reduce_fusion.source_ref
  5.5 43.8 %reduce_to_owners.1 = bf16[2,2,4,2,32,512]{5,4,3,2,1,0:T(8,128)(2,1)} custom-call(s32[32]{0:T(128)} %select_reduce_fusion.source_ref, bf16[11,2,4,2,32,512]{5,4,3,2,1,0:T(8,128)(2,1)} %bitcast.30), custom_call_target="tpu_custom_call" | custom-call | tf_op jit(solution)/shard_map/reduce_to_owners/pallas_call | solution.py:228
  49.3 11.5 %slot_step.1 = (f32[2,512,512]{2,1,0:T(8,128)}, f32[2,512,512]{2,1,0:T(8,128)}, f32[2,512,512]{2,1,0:T(8,128)}, bf16[2,512,512]{2,1,0:T(8,128)(2,1)}, f32[8,128]{1,0:T(8,128)}) custom-call(s32[2]{0:T(128)} %fusion.2.param_ref, bf16[2,512,512]{2,1,0:T(8,128)(2,1)} %bitcast.31, bf16[2,512,512]{2,1,0:T(8,128)(2,1)} %bitcast.35, bf16[2,512,512]{2,1,0:T(8,128)(2,1)} %bitcast.36, ...), custom_call_target="tpu_custom_call" | custom-call | tf_op jit(solution)/shard_map/slot_step/pallas_call | solution.py:309
  60.8 48.6 %gather_blocks.1 = (bf16[11,2,4,2,32,512]{5,4,3,2,1,0:T(8,128)(2,1)}, f32[8,128]{1,0:T(8,128)}) custom-call(s32[11]{0:T(128)} %multiply_add_fusion.place_ref, f32[8,128]{1,0:T(8,128)} %get-tuple-element.14.norm_ref, bf16[2,2,4,2,32,512]{5,4,3,2,1,0:T(8,128)(2,1)} %bitcast.37), custom_call_target="tpu_custom_call" | custom-call | tf_op jit(solution)/shard_map/gather_blocks/pallas_call | solution.py:464
  109.4 0.8 sqrt_bitcast_fusion
  110.1 0.1 select_reduce_fusion.2
  110.2 6.9 %fusion = bf16[11,512,512]{2,1,0:T(8,128)(2,1)} fusion(bf16[11,2,4,2,32,512]{5,4,3,2,1,0:T(8,128)(2,1)} %get-tuple-element.17, f32[11]{0:T(128)S(1)} %select_reduce_fusion.2), kind=kLoop, calls=%fused_computation.1 | loop fusion | flops 8650752 | bytes 11534380 | tf_op jit(solution)/shard_map/convert_element_type | solution.py:525
  (1 shorter events, 0.0 us)

commit v2 on v1

v2 whole, which is shorter than its diff:
```python
import functools

import jax
import jax.numpy as jnp
from jax import lax
from jax.experimental import pallas as pl
from jax.experimental.pallas import tpu as pltpu
from jax.sharding import PartitionSpec as P

DECAY = 0.95
TINY = 1e-06
NY, NX, NC = 4, 2, 2
GRANT = 30 << 20
BF = jnp.bfloat16
F32 = jnp.float32


def position():
    d = lax.axis_index("dp")
    return d // 4, (d // 2) % 2, d % 2


def flat(y, x, c):
    return (y % NY) * 4 + (x % NX) * 2 + c % NC


OFFSETS = [
    (dy, dx, dc)
    for dy in (2, 1, 3, 0)
    for dx in (1, 0)
    for dc in (0, 1)
    if (dy, dx, dc) != (0, 0, 0)
]


def slot_places(owner_ref, nblk):
    owners = [owner_ref[0, b] for b in range(nblk)]
    places = []
    for b in range(nblk):
        place = owners[b] * 2
        for other in range(b):
            place = place + jnp.where(owners[other] == owners[b], 1, 0)
        places.append(place)
    return places


class Copies:
    def __init__(self, send, recv):
        self.send, self.recv, self.count, self.all = send, recv, 0, []

    def start(self, src, dst, where):
        i = self.count
        self.count += 1
        copy = pltpu.make_async_remote_copy(
            src_ref=src,
            dst_ref=dst,
            send_sem=self.send.at[i],
            recv_sem=self.recv.at[i],
            device_id=where,
            device_id_type=pl.DeviceIdType.MESH,
        )
        copy.start()
        self.all.append(copy)
        return copy

    def finish(self):
        for copy in self.all:
            copy.wait_send()


def add_blocks(count, out, first, second):
    def body(b, carry):
        out[b] = first[b] + second[b]
        return carry

    lax.fori_loop(0, count, body, 0)


def add_many(count, out, *terms):
    def body(b, carry):
        total = terms[0][b].astype(F32)
        for term in terms[1:]:
            total = total + term[b].astype(F32)
        out[b] = total.astype(BF)
        return carry

    lax.fori_loop(0, count, body, 0)


def step_kernel(
    nblk, na_blk, n_shard, owner_hbm, param_hbm, grad_ref, lstat_hbm, rstat_hbm, moment_hbm,
    lroot_hbm, rroot_hbm, nl_ref, nr_ref, nm_ref, out_ref,
    loc, grad, rem, far_a, mid_b, near_a, mid_a, far_b, near_b, share, stage,
    held, lroot, rroot, direct, acc, norm_ref, slots, norms, group, columns,
    source_ref, owner_ref, param_ref, local_sem, state_sem, send_sem, recv_sem,
):
    y, x, c = position()
    mine = flat(y, x, c)
    shard = lax.axis_index("shard")
    nb_blk = nblk - na_blk
    rows = share.shape[1]
    half = rows // 2
    ox, oc = 1 - x, 1 - c
    up, down, across = (y + 1) % NY, (y + 3) % NY, (y + 2) % NY
    A = pl.ds(0, na_blk)
    B = pl.ds(na_blk, nb_blk)
    ALL = pl.ds(0, nblk)
    H = (pl.ds(0, half), pl.ds(half, half))

    def gpart(which, core, buf=grad):
        return [
            buf.at[A, core, across],
            buf.at[B, core, :, ox],
            buf.at[A, core, up],
            buf.at[A, core, down],
            buf.at[B, core, :, x],
            buf.at[A, core, y],
        ][which]

    def vpart(buf, which):
        return [
            buf.at[A, across],
            buf.at[B, :, ox],
            buf.at[A, up],
            buf.at[A, down],
            buf.at[B, :, x],
            buf.at[A, y],
        ][which]

    loads = {}
    for i in range(6):
        for own, core in enumerate((oc, c)):
            load = pltpu.make_async_copy(
                gpart(i, core, grad_ref), gpart(i, core), local_sem.at[i, own]
            )
            load.start()
            loads[i, own] = load
    states = [
        pltpu.make_async_copy(src, dst, state_sem.at[i])
        for i, (src, dst) in enumerate((
            (lroot_hbm, lroot), (rroot_hbm, rroot), (moment_hbm, nm_ref),
            (lstat_hbm, nl_ref), (rstat_hbm, nr_ref),
            (owner_hbm, owner_ref), (param_hbm, param_ref),
        ))
    ]
    for load in states:
        load.start()

    barrier = pltpu.get_barrier_semaphore()
    for dy, dx, dc in OFFSETS:
        pl.semaphore_signal(
            barrier, inc=1, device_id={"dp": flat(y + dy, x + dx, c + dc)},
            device_id_type=pl.DeviceIdType.MESH,
        )
    for k in range(1, n_shard):
        pl.semaphore_signal(
            barrier, inc=1, device_id={"shard": (shard + k) % n_shard},
            device_id_type=pl.DeviceIdType.MESH,
        )
    pl.semaphore_wait(barrier, len(OFFSETS) + n_shard - 1)

    to_core = {"dp": flat(y, x, oc)}
    to_x = {"dp": flat(y, ox, c)}
    to_up = {"dp": flat(up, x, c)}
    to_down = {"dp": flat(down, x, c)}
    copies = Copies(send_sem, recv_sem)
    pair = []
    for i in range(6):
        loads[i, 0].wait()
        pair.append(copies.start(gpart(i, oc), vpart(rem, i), to_core))

    def pair_sum(i):
        loads[i, 1].wait()
        pair[i].wait_recv()
        out, mine, other = vpart(loc, i), gpart(i, c), vpart(rem, i)
        inner = mine.shape[1]
        for j in range(inner):
            add_blocks(out.shape[0], out.at[:, j], mine.at[:, j], other.at[:, j])

    pair_sum(0)
    fa = [
        copies.start(loc.at[A, across, 0], far_a.at[0], to_up),
        copies.start(loc.at[A, across, 1], far_a.at[1], to_down),
    ]
    pair_sum(1)
    mb = [
        copies.start(loc.at[B, chunk, ox], mid_b.at[:, chunk], to_x)
        for chunk in (across, up, down, y)
    ]
    pair_sum(2)
    n_a = {(0, 1): copies.start(loc.at[A, up, 1], near_a.at[0, 1], to_up)}
    pair_sum(3)
    n_a[1, 0] = copies.start(loc.at[A, down, 0], near_a.at[1, 0], to_down)
    pair_sum(4)
    pair_sum(5)

    for load in states[5:]:
        load.wait()
    places = slot_places(owner_ref, nblk)

    def find(slot, carry):
        block = nblk
        for b in range(nblk):
            block = jnp.where(places[b] == slot, b, block)
        source_ref[slot] = block
        return carry

    lax.fori_loop(0, 2 * NY * NX * NC, find, 0)

    fa[0].wait_recv()
    add_blocks(na_blk, loc.at[A, up, 0], loc.at[A, up, 0], far_a.at[0])
    n_a[0, 0] = copies.start(loc.at[A, up, 0], near_a.at[0, 0], to_up)
    fa[1].wait_recv()
    add_blocks(na_blk, loc.at[A, down, 1], loc.at[A, down, 1], far_a.at[1])
    n_a[1, 1] = copies.start(loc.at[A, down, 1], near_a.at[1, 1], to_down)

    def middle(i, chunk):
        mb[i].wait_recv()
        add_blocks(nb_blk, loc.at[B, chunk, x], loc.at[B, chunk, x], mid_b.at[:, chunk])

    middle(0, across)
    fb = [
        copies.start(loc.at[B, across, x, H[0]], far_b.at[0], to_up),
        copies.start(loc.at[B, across, x, H[1]], far_b.at[1], to_down),
    ]
    middle(1, up)
    n_b = {(0, 1): copies.start(loc.at[B, up, x, H[1]], near_b.at[0, 1], to_up)}
    middle(2, down)
    n_b[1, 0] = copies.start(loc.at[B, down, x, H[0]], near_b.at[1, 0], to_down)

    for key in ((0, 1), (1, 0), (0, 0), (1, 1)):
        n_a[key].wait_recv()
    add_many(na_blk, loc.at[A, y, ox], loc.at[A, y, ox], near_a.at[0, ox], near_a.at[1, ox])
    ma = copies.start(loc.at[A, y, ox], mid_a, to_x)

    fb[0].wait_recv()
    add_blocks(nb_blk, loc.at[B, up, x, H[0]], loc.at[B, up, x, H[0]], far_b.at[0])
    n_b[0, 0] = copies.start(loc.at[B, up, x, H[0]], near_b.at[0, 0], to_up)
    fb[1].wait_recv()
    add_blocks(nb_blk, loc.at[B, down, x, H[1]], loc.at[B, down, x, H[1]], far_b.at[1])
    n_b[1, 1] = copies.start(loc.at[B, down, x, H[1]], near_b.at[1, 1], to_down)

    share[nblk] = jnp.zeros(share.shape[1:], BF)
    ma.wait_recv()
    add_many(
        na_blk, share.at[A], loc.at[A, y, x], near_a.at[0, x], near_a.at[1, x], mid_a
    )
    mb[3].wait_recv()
    for key in ((0, 1), (1, 0), (0, 0), (1, 1)):
        n_b[key].wait_recv()
    for h in range(2):
        add_many(
            nb_blk, share.at[B, H[h]], loc.at[B, y, x, H[h]], mid_b.at[:, y, H[h]],
            near_b.at[0, h], near_b.at[1, h],
        )

    sent = []
    for k, (dy, dx, dc) in enumerate(OFFSETS):
        q = flat(y + dy, x + dx, c + dc)
        for j in range(2):
            stage[k, j] = share[source_ref[q * 2 + j]]
        sent.append(copies.start(stage.at[k], held.at[:, c, y, x], {"dp": q}))
    for j in range(2):
        held[j, c, y, x] = share[source_ref[mine * 2 + j]]
    for load in states[:3]:
        load.wait()
    for copy in sent:
        copy.wait_recv()

    step = 2 * NX * rows
    width = held.shape[-1]
    block = 4 * step

    def whole(j):
        return held[j].reshape(block, width)

    def strip_of(j, r):
        return held[j, r // 2, pl.ds(2 * (r % 2), 2)].reshape(step, width)

    acc[...] = jnp.zeros_like(acc)

    def precondition(i, carry):
        j, r = i // 4, i % 4
        at = pl.ds(pl.multiple_of(r * step, step), step)
        left = jnp.dot(lroot[j, at], whole(j), preferred_element_type=F32)
        high = left.astype(BF)
        low = (left - high.astype(F32)).astype(BF)
        direction = jnp.dot(high, rroot[j], preferred_element_type=F32)
        direction += jnp.dot(low, rroot[j], preferred_element_type=F32)
        part = direction.astype(BF).reshape(2, NX, rows, width)
        direct[j, r // 2, pl.ds(2 * (r % 2), 2)] = part
        wide = strip_of(j, r).astype(F32)
        moment = DECAY * nm_ref[j, at] + (1.0 - DECAY) * (wide * wide)
        nm_ref[j, at] = moment
        adam = wide / (jnp.sqrt(moment) + TINY)
        acc[j, 0] += jnp.sum((adam * adam).reshape(step // 8, 8, width), axis=0)
        acc[j, 1] += jnp.sum((direction * direction).reshape(step // 8, 8, width), axis=0)
        return carry

    lax.fori_loop(0, 8, precondition, 0)

    tile = (8, 128)
    row = lax.broadcasted_iota(jnp.int32, tile, 0)
    lane = lax.broadcasted_iota(jnp.int32, tile, 1)
    local = jnp.zeros(tile, F32)
    for j in range(2):
        block_at = source_ref[mine * 2 + j]
        param = param_ref[shard * nblk + jnp.minimum(block_at, nblk - 1)]
        param = jnp.where(block_at < nblk, param, -1)
        sums = jnp.where(row == 0, jnp.sum(acc[j, 0]), jnp.sum(acc[j, 1]))
        local = local + jnp.where((lane == param) & (row < 2), sums, 0.0)
    norm_ref[...] = local

    first, second = [], []
    for dy, dx, dc in OFFSETS:
        q = flat(y + dy, x + dx, c + dc)
        first.append(copies.start(norm_ref, norms.at[mine], {"dp": q}))
    for dy, dx, dc in OFFSETS:
        qy, qx, qc = (y + dy) % NY, (x + dx) % NX, (c + dc) % NC
        second.append(
            copies.start(direct.at[:, qc, qy, qx], slots.at[mine], {"dp": flat(qy, qx, qc)})
        )
    norms[mine] = norm_ref[...]
    slots[mine] = direct[:, c, y, x]
    for load in states[3:5]:
        load.wait()

    def gram(i, carry):
        j, r = i // 4, i % 4
        at = pl.ds(pl.multiple_of(r * step, step), step)
        left = lax.dot_general(
            strip_of(j, r), whole(j), (((1,), (1,)), ((), ())), preferred_element_type=F32
        )
        nl_ref[j, at] = DECAY * nl_ref[j, at] + (1.0 - DECAY) * left
        columns_of = held[j, :, :, :, :, at].reshape(block, step)
        right = lax.dot_general(
            columns_of, whole(j), (((0,), (0,)), ((), ())), preferred_element_type=F32
        )
        nr_ref[j, at] = DECAY * nr_ref[j, at] + (1.0 - DECAY) * right
        return carry

    lax.fori_loop(0, 2, gram, 0)
    for copy in first:
        copy.wait_recv()
    total = norms[0]
    for i in range(1, norms.shape[0]):
        total = total + norms[i]
    group[...] = total
    third = [
        copies.start(group, columns.at[shard], {"shard": (shard + k) % n_shard})
        for k in range(1, n_shard)
    ]
    columns[shard] = total

    lax.fori_loop(2, 8, gram, 0)

    for copy in third:
        copy.wait_recv()
    total = columns[0]
    for i in range(1, n_shard):
        total = total + columns[i]
    ratio = jnp.sqrt((total[0:1] + TINY) / (total[1:2] + TINY))
    for copy in second:
        copy.wait_recv()
    for b in range(nblk):
        place = places[b]
        param = param_ref[shard * nblk + b]
        scale = jnp.sum(jnp.where(lane[0:1] == param, ratio, 0.0), axis=1, keepdims=True)
        out_ref[b, c, y, x] = (scale * slots[place // 2, place % 2].astype(F32)).astype(BF)

    arrivals = []

    def pass_on(where, *index):
        part = out_ref.at[index]
        return copies.start(part, part, where)

    def across_cores(*index):
        arrivals.append(pass_on(to_core, *index))

    xa = pass_on(to_x, A, c, y, x)
    b_near = [pass_on(to_up, B, c, y, x), pass_on(to_down, B, c, y, x)]
    xb = [pass_on(to_x, B, c, y, x)]
    a_near = [pass_on(to_up, A, c, y, x), pass_on(to_down, A, c, y, x)]
    across_cores(ALL, c, y, x)

    b_near[0].wait_recv()
    b_far = [pass_on(to_up, B, c, down, x, H[0])]
    xb.append(pass_on(to_x, B, c, down, x))
    b_near[1].wait_recv()
    b_far.append(pass_on(to_down, B, c, up, x, H[1]))
    xb.append(pass_on(to_x, B, c, up, x))
    across_cores(B, c, down, x)
    across_cores(B, c, up, x)

    xa.wait_recv()
    a_next = [pass_on(to_up, A, c, y, ox), pass_on(to_down, A, c, y, ox)]
    across_cores(A, c, y, ox)

    a_near[0].wait_recv()
    a_far = [pass_on(to_up, A, c, down, x)]
    across_cores(A, c, down, x)
    a_near[1].wait_recv()
    across_cores(A, c, up, x)

    b_far[0].wait_recv()
    b_far[1].wait_recv()
    xb.append(pass_on(to_x, B, c, across, x))
    across_cores(B, c, across, x)

    a_next[1].wait_recv()
    a_far.append(pass_on(to_down, A, c, up, ox))
    across_cores(A, c, up, ox)
    a_next[0].wait_recv()
    across_cores(A, c, down, ox)

    for i, chunk in enumerate((y, down, up)):
        xb[i].wait_recv()
        across_cores(B, c, chunk, ox)
    a_far[0].wait_recv()
    across_cores(A, c, across, x)
    a_far[1].wait_recv()
    across_cores(A, c, across, ox)
    xb[3].wait_recv()
    across_cores(B, c, across, ox)
    for copy in arrivals:
        copy.wait_recv()
    copies.finish()


def flush_kernel(*refs):
    count = len(refs) // 2
    sem = refs[-1]
    copies = [
        pltpu.make_async_copy(refs[i], refs[count + i], sem.at[i]) for i in range(count)
    ]
    for copy in copies:
        copy.start()
    for copy in copies:
        copy.wait()


def flush(*arrays):
    return pl.pallas_call(
        flush_kernel,
        out_shape=tuple(jax.ShapeDtypeStruct(a.shape, a.dtype) for a in arrays),
        in_specs=[pl.BlockSpec(memory_space=pltpu.VMEM)] * len(arrays),
        out_specs=tuple(pl.BlockSpec(memory_space=pltpu.HBM) for _ in arrays),
        scratch_shapes=[pltpu.SemaphoreType.DMA((len(arrays),))],
        compiler_params=pltpu.CompilerParams(vmem_limit_bytes=GRANT),
        name="flush",
    )(*arrays)


def on_device(gradients, owners, block_param, left_stat, right_stat, moment, left_root, right_root):
    _, nblk, block, width = gradients.shape
    n_shard = lax.axis_size("shard")
    n_dev = NY * NX * NC
    rows = block // n_dev
    na_blk = (nblk + 1) // 2
    nb_blk = nblk - na_blk
    n_copies = 23 + 3 * len(OFFSETS) + n_shard - 1 + 15 + 15
    state = jax.ShapeDtypeStruct((2, block, width), F32)
    hbm = pl.BlockSpec(memory_space=pltpu.HBM)
    vmem = pl.BlockSpec(memory_space=pltpu.VMEM)
    slot_rows = (2, NC, NY, NX, rows, width)
    new_left, new_right, new_moment, update = pl.pallas_call(
        functools.partial(step_kernel, nblk, na_blk, n_shard),
        out_shape=(
            state, state, state,
            jax.ShapeDtypeStruct((nblk, NC, NY, NX, rows, width), BF),
        ),
        in_specs=[hbm] * 8,
        out_specs=(vmem, vmem, vmem, vmem),
        scratch_shapes=[
            pltpu.VMEM((nblk, NY, NX, rows, width), BF),
            pltpu.VMEM((nblk, NC, NY, NX, rows, width), BF),
            pltpu.VMEM((nblk, NY, NX, rows, width), BF),
            pltpu.VMEM((2, na_blk, rows, width), BF),
            pltpu.VMEM((nb_blk, NY, rows, width), BF),
            pltpu.VMEM((2, 2, na_blk, rows, width), BF),
            pltpu.VMEM((na_blk, rows, width), BF),
            pltpu.VMEM((2, nb_blk, rows // 2, width), BF),
            pltpu.VMEM((2, 2, nb_blk, rows // 2, width), BF),
            pltpu.VMEM((nblk + 1, rows, width), BF),
            pltpu.VMEM((len(OFFSETS), 2, rows, width), BF),
            pltpu.VMEM(slot_rows, BF),
            pltpu.VMEM((2, block, width), BF),
            pltpu.VMEM((2, block, width), BF),
            pltpu.VMEM(slot_rows, BF),
            pltpu.VMEM((2, 2, 8, width), F32),
            pltpu.VMEM((8, 128), F32),
            pltpu.VMEM((n_dev, 2, rows, width), BF),
            pltpu.VMEM((n_dev, 8, 128), F32),
            pltpu.VMEM((8, 128), F32),
            pltpu.VMEM((n_shard, 8, 128), F32),
            pltpu.SMEM((2 * n_dev,), jnp.int32),
            pltpu.SMEM(owners.shape, jnp.int32),
            pltpu.SMEM(block_param.shape, jnp.int32),
            pltpu.SemaphoreType.DMA((6, 2)),
            pltpu.SemaphoreType.DMA((7,)),
            pltpu.SemaphoreType.DMA((n_copies,)),
            pltpu.SemaphoreType.DMA((n_copies,)),
        ],
        compiler_params=pltpu.CompilerParams(
            collective_id=0, has_side_effects=True, vmem_limit_bytes=GRANT
        ),
        name="shampoo_step",
    )(
        *(
            pltpu.with_memory_space_constraint(array, pltpu.HBM)
            for array in (
                owners, block_param,
                gradients.reshape(nblk, NC, NY, NX, rows, width),
                left_stat[:, 0], right_stat[:, 0], moment[:, 0], left_root[:, 0], right_root[:, 0],
            )
        ),
    )
    new_left, new_right, new_moment, update = flush(new_left, new_right, new_moment, update)
    return (
        new_left[:, None], new_right[:, None], new_moment[:, None],
        update.reshape(nblk, block, width),
    )


def solution(mesh):
    state = P("dp", "shard", None, None)
    return jax.shard_map(
        on_device,
        mesh=mesh,
        in_specs=(state, P("shard", None), P(), state, state, state, state, state),
        out_specs=(state, state, state, P("shard", None, None)),
        check_vma=False,
    )
```

time: 118 us -> 95.3 us (0.81)
  other arithmetic: 11.9 us -> 0 us
  Pallas kernels: 104 us -> 94.5 us
    pallas_call x3 -> x2, Pallas kernels: 104 us -> 94.5 us  [the longest x1 90 us: on_device(): pl.pallas_call(functools.partial(step_kernel, nblk, na_blk, n_shard), out...]
    convert_element_type x1 -> x0, other arithmetic: 6.93 us -> none  [on_device(): update = (block_ratio[:, None, None] * gathered.astype(F32)).astype(BF)]
    add x2 -> x0, other arithmetic: 1.23 us -> none  [the longest x1 1.22 us: on_device(): owner_row * capacity]
where the time goes in v2:
time: 95.3 us; the launch traced here: 95.2 us
  Pallas kernels  94.5 us (99%)
    pallas_call x1, Pallas kernels, on_device(): pl.pallas_call(functools.partial(step_kernel, nblk, na_blk, n_shard), out...  90 us
    pallas_call x1, Pallas kernels, flush(): pl.pallas_call(flush_kernel, out_shape=tuple((jax.ShapeDtypeStruct(a.shap...  4.58 us

profile of v2, /device:TPU:1, one launch (start us, length us, event | category | flops | bytes accessed | tf_op | source)
XLA Modules:
  0.0 95.2 jit_solution(1636461463088067119)
XLA Ops:
  0.6 90.0 %shampoo_step.1 = (f32[2,512,512]{2,1,0:T(8,128)S(1)}, f32[2,512,512]{2,1,0:T(8,128)S(1)}, f32[2,512,512]{2,1,0:T(8,128)S(1)}, bf16[11,2,4,2,32,512]{5,4,3,2,1,0:T(8,128)(2,1)S(1)}) custom-call(s32[1,11]{1,0:T(1,128)} %owner_hbm.1, s32[88]{0:T(128)} %param_hbm.1, bf16[11,2,4,2,32,512]{5,4,3,2,1,0:T(8,128)(2,1)} %bitcast.16, f32[2,512,512]{2,1,0:T(8,128)} %bitcast.17, ...), custom_call_target="tpu_custom_call" | custom-call | tf_op jit(solution)/shard_map/shampoo_step/pallas_call | solution.py:466
  90.6 4.6 %flush.1 = (f32[2,512,512]{2,1,0:T(8,128)}, f32[2,512,512]{2,1,0:T(8,128)}, f32[2,512,512]{2,1,0:T(8,128)}, bf16[11,2,4,2,32,512]{5,4,3,2,1,0:T(8,128)(2,1)}) custom-call(f32[2,512,512]{2,1,0:T(8,128)S(1)} %get-tuple-element.12.refs_0_, f32[2,512,512]{2,1,0:T(8,128)S(1)} %get-tuple-element.13.refs_1_, f32[2,512,512]{2,1,0:T(8,128)S(1)} %get-tuple-element.14.refs_2_, ...), custom_call_target="tpu_custom_call" | custom-call | tf_op jit(solution)/shard_map/flush/pallas_call | solution.py:443

commit v3 on v2

--- a/solution.py
+++ b/solution.py
@@ -143,8 +143,6 @@
             (owner_hbm, owner_ref), (param_hbm, param_ref),
         ))
     ]
-    for load in states:
-        load.start()
 
     barrier = pltpu.get_barrier_semaphore()
     for dy, dx, dc in OFFSETS:
@@ -177,6 +175,8 @@
         for j in range(inner):
             add_blocks(out.shape[0], out.at[:, j], mine.at[:, j], other.at[:, j])
 
+    for load in states:
+        load.start()
     pair_sum(0)
     fa = [
         copies.start(loc.at[A, across, 0], far_a.at[0], to_up),
@@ -254,19 +254,15 @@
             near_b.at[0, h], near_b.at[1, h],
         )
 
-    sent = []
-    for k, (dy, dx, dc) in enumerate(OFFSETS):
-        q = flat(y + dy, x + dx, c + dc)
-        for j in range(2):
+    sent = ([], [])
+    for j in range(2):
+        for k, (dy, dx, dc) in enumerate(OFFSETS):
+            q = flat(y + dy, x + dx, c + dc)
             stage[k, j] = share[source_ref[q * 2 + j]]
-        sent.append(copies.start(stage.at[k], held.at[:, c, y, x], {"dp": q}))
-    for j in range(2):
+            sent[j].append(copies.start(stage.at[k, j], held.at[j, c, y, x], {"dp": q}))
         held[j, c, y, x] = share[source_ref[mine * 2 + j]]
     for load in states[:3]:
         load.wait()
-    for copy in sent:
-        copy.wait_recv()
-
     step = 2 * NX * rows
     width = held.shape[-1]
     block = 4 * step
@@ -279,25 +275,41 @@
 
     acc[...] = jnp.zeros_like(acc)
 
-    def precondition(i, carry):
-        j, r = i // 4, i % 4
-        at = pl.ds(pl.multiple_of(r * step, step), step)
+    def precondition(j, r, carry):
+        tall = 2 * step
+        at = pl.ds(pl.multiple_of(r * tall, tall), tall)
         left = jnp.dot(lroot[j, at], whole(j), preferred_element_type=F32)
         high = left.astype(BF)
         low = (left - high.astype(F32)).astype(BF)
         direction = jnp.dot(high, rroot[j], preferred_element_type=F32)
         direction += jnp.dot(low, rroot[j], preferred_element_type=F32)
-        part = direction.astype(BF).reshape(2, NX, rows, width)
-        direct[j, r // 2, pl.ds(2 * (r % 2), 2)] = part
-        wide = strip_of(j, r).astype(F32)
+        direct[j, r] = direction.astype(BF).reshape(NY, NX, rows, width)
+        wide = held[j, r].reshape(tall, width).astype(F32)
         moment = DECAY * nm_ref[j, at] + (1.0 - DECAY) * (wide * wide)
         nm_ref[j, at] = moment
         adam = wide / (jnp.sqrt(moment) + TINY)
-        acc[j, 0] += jnp.sum((adam * adam).reshape(step // 8, 8, width), axis=0)
-        acc[j, 1] += jnp.sum((direction * direction).reshape(step // 8, 8, width), axis=0)
+        acc[j, 0] += jnp.sum((adam * adam).reshape(tall // 8, 8, width), axis=0)
+        acc[j, 1] += jnp.sum((direction * direction).reshape(tall // 8, 8, width), axis=0)
         return carry
 
-    lax.fori_loop(0, 8, precondition, 0)
+    second = []
+
+    def send_out(j):
+        for dy, dx, dc in OFFSETS:
+            qy, qx, qc = (y + dy) % NY, (x + dx) % NX, (c + dc) % NC
+            second.append(
+                copies.start(
+                    direct.at[j, qc, qy, qx], slots.at[mine, j], {"dp": flat(qy, qx, qc)}
+                )
+            )
+
+    for copy in sent[0]:
+        copy.wait_recv()
+    lax.fori_loop(0, 2, functools.partial(precondition, 0), 0)
+    send_out(0)
+    for copy in sent[1]:
+        copy.wait_recv()
+    lax.fori_loop(0, 2, functools.partial(precondition, 1), 0)
 
     tile = (8, 128)
     row = lax.broadcasted_iota(jnp.int32, tile, 0)
@@ -311,15 +323,11 @@
         local = local + jnp.where((lane == param) & (row < 2), sums, 0.0)
     norm_ref[...] = local
 
-    first, second = [], []
+    first = []
     for dy, dx, dc in OFFSETS:
         q = flat(y + dy, x + dx, c + dc)
         first.append(copies.start(norm_ref, norms.at[mine], {"dp": q}))
-    for dy, dx, dc in OFFSETS:
-        qy, qx, qc = (y + dy) % NY, (x + dx) % NX, (c + dc) % NC
-        second.append(
-            copies.start(direct.at[:, qc, qy, qx], slots.at[mine], {"dp": flat(qy, qx, qc)})
-        )
+    send_out(1)
     norms[mine] = norm_ref[...]
     slots[mine] = direct[:, c, y, x]
     for load in states[3:5]:
@@ -397,9 +405,10 @@
     across_cores(A, c, y, ox)
 
     a_near[0].wait_recv()
-    a_far = [pass_on(to_up, A, c, down, x)]
+    a_far = [pass_on(to_up, A, c, down, x, H[0])]
     across_cores(A, c, down, x)
     a_near[1].wait_recv()
+    a_far.append(pass_on(to_down, A, c, up, x, H[1]))
     across_cores(A, c, up, x)
 
     b_far[0].wait_recv()
@@ -407,18 +416,21 @@
     xb.append(pass_on(to_x, B, c, across, x))
     across_cores(B, c, across, x)
 
+    a_next[0].wait_recv()
+    a_far.append(pass_on(to_up, A, c, down, ox, H[0]))
+    across_cores(A, c, down, ox)
     a_next[1].wait_recv()
-    a_far.append(pass_on(to_down, A, c, up, ox))
+    a_far.append(pass_on(to_down, A, c, up, ox, H[1]))
     across_cores(A, c, up, ox)
-    a_next[0].wait_recv()
-    across_cores(A, c, down, ox)
 
     for i, chunk in enumerate((y, down, up)):
         xb[i].wait_recv()
         across_cores(B, c, chunk, ox)
     a_far[0].wait_recv()
+    a_far[1].wait_recv()
     across_cores(A, c, across, x)
-    a_far[1].wait_recv()
+    a_far[2].wait_recv()
+    a_far[3].wait_recv()
     across_cores(A, c, across, ox)
     xb[3].wait_recv()
     across_cores(B, c, across, ox)
@@ -458,7 +470,7 @@
     rows = block // n_dev
     na_blk = (nblk + 1) // 2
     nb_blk = nblk - na_blk
-    n_copies = 23 + 3 * len(OFFSETS) + n_shard - 1 + 15 + 15
+    n_copies = 23 + 5 * len(OFFSETS) + n_shard - 1 + 17 + 15
     state = jax.ShapeDtypeStruct((2, block, width), F32)
     hbm = pl.BlockSpec(memory_space=pltpu.HBM)
     vmem = pl.BlockSpec(memory_space=pltpu.VMEM)

time: 95.3 us -> 90.1 us (0.945)
  Pallas kernels: 94.5 us -> 89.3 us
    pallas_call x1, Pallas kernels: 90 us -> 84.7 us  [on_device(): pl.pallas_call(functools.partial(step_kernel, nblk, na_blk, n_shard), out...]
where the time goes in v3:
time: 90.1 us; the launch traced here: 90 us
  Pallas kernels  89.3 us (99%)
    pallas_call x1, Pallas kernels, on_device(): pl.pallas_call(functools.partial(step_kernel, nblk, na_blk, n_shard), out...  84.7 us
    pallas_call x1, Pallas kernels, flush(): pl.pallas_call(flush_kernel, out_shape=tuple((jax.ShapeDtypeStruct(a.shap...  4.58 us

profile of v3, /device:TPU:1, one launch (start us, length us, event | category | flops | bytes accessed | tf_op | source)
XLA Modules:
  0.0 90.0 jit_solution(12254201828240235237)
XLA Ops:
  0.6 84.7 %shampoo_step.1 = (f32[2,512,512]{2,1,0:T(8,128)S(1)}, f32[2,512,512]{2,1,0:T(8,128)S(1)}, f32[2,512,512]{2,1,0:T(8,128)S(1)}, bf16[11,2,4,2,32,512]{5,4,3,2,1,0:T(8,128)(2,1)S(1)}) custom-call(s32[1,11]{1,0:T(1,128)} %owner_hbm.1, s32[88]{0:T(128)} %param_hbm.1, bf16[11,2,4,2,32,512]{5,4,3,2,1,0:T(8,128)(2,1)} %bitcast.16, f32[2,512,512]{2,1,0:T(8,128)} %bitcast.17, ...), custom_call_target="tpu_custom_call" | custom-call | tf_op jit(solution)/shard_map/shampoo_step/pallas_call | solution.py:478
  85.4 4.6 %flush.1 = (f32[2,512,512]{2,1,0:T(8,128)}, f32[2,512,512]{2,1,0:T(8,128)}, f32[2,512,512]{2,1,0:T(8,128)}, bf16[11,2,4,2,32,512]{5,4,3,2,1,0:T(8,128)(2,1)}) custom-call(f32[2,512,512]{2,1,0:T(8,128)S(1)} %get-tuple-element.12.refs_0_, f32[2,512,512]{2,1,0:T(8,128)S(1)} %get-tuple-element.13.refs_1_, f32[2,512,512]{2,1,0:T(8,128)S(1)} %get-tuple-element.14.refs_2_, ...), custom_call_target="tpu_custom_call" | custom-call | tf_op jit(solution)/shard_map/flush/pallas_call | solution.py:455

commit v4 on v3

--- a/solution.py
+++ b/solution.py
@@ -26,7 +26,7 @@
 
 OFFSETS = [
     (dy, dx, dc)
-    for dy in (2, 1, 3, 0)
+    for dy in (1, 3, 2, 0)
     for dx in (1, 0)
     for dc in (0, 1)
     if (dy, dx, dc) != (0, 0, 0)
@@ -442,9 +442,15 @@
 def flush_kernel(*refs):
     count = len(refs) // 2
     sem = refs[-1]
-    copies = [
-        pltpu.make_async_copy(refs[i], refs[count + i], sem.at[i]) for i in range(count)
-    ]
+    copies = []
+    for i in range(count):
+        length = refs[i].shape[0]
+        for part in range(length):
+            copies.append(
+                pltpu.make_async_copy(
+                    refs[i].at[part], refs[count + i].at[part], sem.at[len(copies)]
+                )
+            )
     for copy in copies:
         copy.start()
     for copy in copies:
@@ -457,7 +463,7 @@
         out_shape=tuple(jax.ShapeDtypeStruct(a.shape, a.dtype) for a in arrays),
         in_specs=[pl.BlockSpec(memory_space=pltpu.VMEM)] * len(arrays),
         out_specs=tuple(pl.BlockSpec(memory_space=pltpu.HBM) for _ in arrays),
-        scratch_shapes=[pltpu.SemaphoreType.DMA((len(arrays),))],
+        scratch_shapes=[pltpu.SemaphoreType.DMA((sum(a.shape[0] for a in arrays),))],
         compiler_params=pltpu.CompilerParams(vmem_limit_bytes=GRANT),
         name="flush",
     )(*arrays)

time: 90.1 us -> 89.3 us (level)
  no operation moved by 1% of the time
where the time goes in v4:
time: 89.3 us; the launch traced here: 89.2 us
  Pallas kernels  88.5 us (99%)
    pallas_call x1, Pallas kernels, on_device(): pl.pallas_call(functools.partial(step_kernel, nblk, na_blk, n_shard), out...  84 us
    pallas_call x1, Pallas kernels, flush(): pl.pallas_call(flush_kernel, out_shape=tuple((jax.ShapeDtypeStruct(a.shap...  4.53 us

profile of v4, /device:TPU:1, one launch (start us, length us, event | category | flops | bytes accessed | tf_op | source)
XLA Modules:
  0.0 89.2 jit_solution(15460263608974086320)
XLA Ops:
  0.6 84.0 %shampoo_step.1 = (f32[2,512,512]{2,1,0:T(8,128)S(1)}, f32[2,512,512]{2,1,0:T(8,128)S(1)}, f32[2,512,512]{2,1,0:T(8,128)S(1)}, bf16[11,2,4,2,32,512]{5,4,3,2,1,0:T(8,128)(2,1)S(1)}) custom-call(s32[1,11]{1,0:T(1,128)} %owner_hbm.1, s32[88]{0:T(128)} %param_hbm.1, bf16[11,2,4,2,32,512]{5,4,3,2,1,0:T(8,128)(2,1)} %bitcast.16, f32[2,512,512]{2,1,0:T(8,128)} %bitcast.17, ...), custom_call_target="tpu_custom_call" | custom-call | tf_op jit(solution)/shard_map/shampoo_step/pallas_call | solution.py:484
  84.6 4.5 %flush.1 = (f32[2,512,512]{2,1,0:T(8,128)}, f32[2,512,512]{2,1,0:T(8,128)}, f32[2,512,512]{2,1,0:T(8,128)}, bf16[11,2,4,2,32,512]{5,4,3,2,1,0:T(8,128)(2,1)}) custom-call(f32[2,512,512]{2,1,0:T(8,128)S(1)} %get-tuple-element.12.refs_0_, f32[2,512,512]{2,1,0:T(8,128)S(1)} %get-tuple-element.13.refs_1_, f32[2,512,512]{2,1,0:T(8,128)S(1)} %get-tuple-element.14.refs_2_, ...), custom_call_target="tpu_custom_call" | custom-call | tf_op jit(solution)/shard_map/flush/pallas_call | solution.py:461
